TPU v7x, 32 devices: a whole 2x2x4 slice. The times are simulated.
32 devices in a mesh: seq: 16 (over z, x, core), tp: 2 (over y).
Axes of the slice: x: 2, y: 2, z: 4, core: 2. Of those that a mesh axis runs over, the one named last changes fastest.
Arguments:
- hidden_in: bfloat16 [2048, 4096], P('seq', 'tp'), may hold values from -64 to 64
- span_order: int32 [16], replicated, may hold values from 0 to 15, each once
- norm_gain: bfloat16 [4096], P('tp'), may hold values from 0.099609375 to 1.8984375
- w_query: bfloat16 [4096, 4096], P('seq', 'tp'), may hold values from -0.09375 to 0.09375
- bias_query: bfloat16 [4096], P('tp'), may hold values from -14 to 14
- key_value_weight: bfloat16 [4096, 2, 1024], P('seq', None, 'tp'), may hold values from -0.09375 to 0.09375
- bias_kv: bfloat16 [2, 1024], P(None, 'tp'), may hold values from -14 to 14
- w_out: bfloat16 [4096, 4096], P('tp', 'seq'), may hold values from -0.09375 to 0.09375
- post_gain: bfloat16 [4096], P('tp'), may hold values from 0.099609375 to 1.8984375
Outputs:
- attn_out: bfloat16 [2048, 4096], P('seq', 'tp')
- normed: bfloat16 [2048, 4096], P('seq', 'tp')
Inputs may be any that keep to these rules, and one draw needn't show every extreme that they name: Each span number appears once; row r of hidden_in belongs to span span_order[r // 128].
All inputs are finite; a program needn't handle non-finite values.
Results may differ from a plain program's by a relative error of at most 0.014.
Values may be sent and summed in bfloat16 or wider, within the bound.
A program may use at most 128 MiB of HBM per device.

v0:
```python
import math
import jax
import jax.numpy as jnp
from jax import lax
from jax.sharding import PartitionSpec as P

MODEL_WIDTH = 4096
HEAD_SIZE = 128
GROUP = 4
eps = 1e-06
rope_base = 1000000.0


def apply_rotary(field, token_positions):
    half = field.shape[-1] // 2
    inverse = jnp.exp(-math.log(rope_base) * jnp.arange(half, dtype=jnp.float32) / half)
    angles = token_positions.astype(jnp.float32)[:, None] * inverse[None, :]
    cosine = jnp.cos(angles)[:, None, :]
    sine = jnp.sin(angles)[:, None, :]
    first = field[..., :half]
    second = field[..., half:]
    return jnp.concatenate(
        [first * cosine - second * sine, second * cosine + first * sine], axis=-1
    )


def span_lookup(order, devices):
    table_ids = jnp.arange(order.shape[0], dtype=jnp.int32)
    return jnp.sum(jnp.where(devices[:, None] == table_ids[None, :], order[None, :], 0), axis=1)


def per_device(
    hidden_in,
    span_order,
    norm_gain,
    w_query,
    bias_query,
    key_value_weight,
    bias_kv,
    w_out,
    post_gain,
):
    tok_rows = hidden_in.shape[0]
    seq_index = lax.axis_index("seq")
    own_span = span_lookup(span_order, jnp.full((1,), seq_index, jnp.int32))[0]
    token_positions = own_span * tok_rows + jnp.arange(tok_rows, dtype=jnp.int32)
    local = hidden_in.astype(jnp.float32)
    raw_rows, gains = (
        lax.all_gather(hidden_in, "tp", axis=1, tiled=True),
        lax.all_gather(norm_gain[None, :], "tp", axis=1, tiled=True),
    )
    full_rows = raw_rows.astype(jnp.float32)
    meansq = jnp.mean(full_rows * full_rows, axis=1, keepdims=True)
    normed_in = (full_rows * lax.rsqrt(meansq + eps) * gains.astype(jnp.float32)).astype(
        jnp.bfloat16
    )
    columns = normed_in
    query_proj = jnp.dot(
        columns,
        lax.all_gather(w_query, "seq", axis=0, tiled=True),
        preferred_element_type=jnp.float32,
    )
    columns = normed_in
    pair_proj = jnp.einsum(
        "tr,rkc->tkc",
        columns,
        lax.all_gather(key_value_weight, "seq", axis=0, tiled=True),
        preferred_element_type=jnp.float32,
    )
    query_heads = w_query.shape[1] // HEAD_SIZE
    kv_heads = key_value_weight.shape[2] // HEAD_SIZE
    query_proj = query_proj + bias_query.astype(jnp.float32)[None, :]
    queries = apply_rotary(
        query_proj.reshape(tok_rows, query_heads, HEAD_SIZE), token_positions
    ).astype(jnp.bfloat16)
    pair_proj = pair_proj + bias_kv.astype(jnp.float32)[None, :, :]
    rotated_keys = apply_rotary(
        pair_proj[:, 0, :].reshape(tok_rows, kv_heads, HEAD_SIZE), token_positions
    )
    rotated_keys = rotated_keys.astype(jnp.bfloat16).reshape(tok_rows, kv_heads * HEAD_SIZE)
    value_rows = pair_proj[:, 1, :].astype(jnp.bfloat16)
    grouped = (
        queries.reshape(tok_rows, kv_heads, GROUP, HEAD_SIZE)
        .transpose(1, 2, 0, 3)
        .reshape(kv_heads, GROUP * tok_rows, HEAD_SIZE)
    )
    query_pos = jnp.tile(token_positions, GROUP)
    last_query = jnp.max(token_positions)
    scale = 1.0 / math.sqrt(HEAD_SIZE)
    start_state = (
        jnp.full((kv_heads, GROUP * tok_rows), -1e30, jnp.float32),
        jnp.zeros((kv_heads, GROUP * tok_rows), jnp.float32),
        jnp.zeros((kv_heads, GROUP * tok_rows, HEAD_SIZE), jnp.float32),
    )
    key_piece = lax.all_gather(rotated_keys, "seq", axis=0, tiled=True)
    value_piece = lax.all_gather(value_rows, "seq", axis=0, tiled=True)
    count = key_piece.shape[0]
    block = math.gcd(count, 1536)

    def visit(step, state):
        first = step * block
        key_block = lax.dynamic_slice_in_dim(key_piece, first, block, 0).reshape(
            block, kv_heads, HEAD_SIZE
        )
        value_block = lax.dynamic_slice_in_dim(value_piece, first, block, 0).reshape(
            block, kv_heads, HEAD_SIZE
        )
        row_ids = first + jnp.arange(block, dtype=jnp.int32)
        key_pos = span_lookup(span_order, row_ids // tok_rows) * tok_rows + row_ids % tok_rows

        def update(current):
            maxima, totals, sums = current
            scores = (
                jnp.einsum("kqd,nkd->kqn", grouped, key_block, preferred_element_type=jnp.float32)
                * scale
            )
            allowed = (key_pos[None, :] <= query_pos[:, None])[None, :, :]
            scores = jnp.where(allowed, scores, -1e30)
            fresh = jnp.maximum(maxima, jnp.max(scores, axis=2))
            weights = jnp.where(allowed, jnp.exp(scores - fresh[:, :, None]), 0.0)
            factor = jnp.exp(maxima - fresh)
            totals = totals * factor + jnp.sum(weights, axis=2)
            sums = sums * factor[:, :, None] + jnp.einsum(
                "kqn,nkd->kqd",
                weights.astype(jnp.bfloat16),
                value_block,
                preferred_element_type=jnp.float32,
            )
            return (fresh, totals, sums)

        return lax.cond(jnp.min(key_pos) <= last_query, update, lambda current: current, state)

    maxima, totals, sums = lax.fori_loop(0, count // block, visit, start_state)
    attended = (sums / totals[:, :, None]).astype(jnp.bfloat16)
    attended = (
        attended.reshape(kv_heads, GROUP, tok_rows, HEAD_SIZE)
        .transpose(2, 0, 1, 3)
        .reshape(tok_rows, query_heads * HEAD_SIZE)
    )
    partial_out = jnp.dot(
        attended,
        lax.all_gather(w_out, "seq", axis=1, tiled=True),
        preferred_element_type=jnp.float32,
    )
    mixed = lax.psum_scatter(
        partial_out.astype(jnp.bfloat16), "tp", scatter_dimension=1, tiled=True
    ).astype(jnp.float32)
    attn_out = mixed.astype(jnp.bfloat16)
    stream = local + mixed
    post_sq = lax.psum(jnp.sum(stream * stream, axis=1), "tp")
    normed = (
        stream
        * lax.rsqrt(post_sq / MODEL_WIDTH + eps)[:, None]
        * post_gain.astype(jnp.float32)[None, :]
    ).astype(jnp.bfloat16)
    return (attn_out, normed)


def solution(mesh):
    placed = (
        P("seq", "tp"),
        P(),
        P("tp"),
        P("seq", "tp"),
        P("tp"),
        P("seq", None, "tp"),
        P(None, "tp"),
        P("tp", "seq"),
        P("tp"),
    )
    return jax.shard_map(
        per_device,
        mesh=mesh,
        in_specs=placed,
        out_specs=(P("seq", "tp"), P("seq", "tp")),
        check_vma=False,
    )
```

profile of v0, /device:TPU:0, one launch (start us, length us, event | category | flops | bytes accessed | tf_op | source)
XLA Modules:
  0.0 499.7 jit_solution(17849845767442077635)
XLA Ops:
  7.2 0.7 all-gather.9.cloned.1.call-update
  7.9 1.9 copy.44
  9.9 5.5 %all-gather = bf16[4096]{0:T(1024)(128)(2,1)S(1)} all-gather(bf16[2048]{0:T(1024)(128)(2,1)} %param.15), channel_id=2, replica_groups=mesh['seq'=16,'tp'=2] {'tp'}, dimensions={0}, use_global_device_ids=true | all-gather | bytes 12288 | tf_op jit(solution)/shard_map/all_gather | solution.py:50
  15.4 0.7 convert_element_type.69
  16.1 17.4 %all-gather.9.cloned.1.call-done = bf16[128,4096]{1,0:T(8,128)(2,1)} async-done(((bf16[128,2048]{1,0:T(8,128)(2,1)}), bf16[128,4096]{1,0:T(8,128)(2,1)}) %all-gather.9.cloned.1.call-update) | async-done | bytes 1048592 | tf_op jit(solution)/shard_map/all_gather | solution.py:49
  33.6 1.5 fusion.18
  35.1 75.6 %all-gather.11.cloned.1.call-done = bf16[4096,2,512]{2,0,1:T(8,128)(2,1)} async-done(((bf16[256,2,512]{2,0,1:T(8,128)(2,1)}), bf16[4096,2,512]{2,0,1:T(8,128)(2,1)}) %all-gather.11.cloned.1.call-update) | async-done | bytes 8388624 | tf_op jit(solution)/shard_map/all_gather | solution.py:67
  110.7 5.0 %convolution_add_fusion.1 = f32[128,2,512]{2,0,1:T(8,128)S(1)} fusion(bf16[4096,2,512]{2,0,1:T(8,128)(2,1)} %all-gather.11.cloned.1.call-done, bf16[128,4096]{1,0:T(8,128)(2,1)} %all-gather.9.cloned.1.call-done, f32[4096]{0:T(1024)S(1)} %mul.210, f32[128]{0:T(128)S(1)} %add_rsqrt_fusion.1, f32[2,512]{1,0:T(2,128)S(1)} %convert_element_type.69), kind=kOutput, calls=%fused_computation.39 | convolution fusion | flops 1075970048 | bytes 9982464 | tf_op jit(solution)/shard_map/tr,rkc->tkc/dot_general | solution.py:64
  115.7 0.7 slice.40
  119.3 0.8 copy.45
  121.5 35.1 %all-gather.19.cloned.1.call-done = bf16[2048,1,512]{2,0,1:T(8,128)(2,1)} async-done(((bf16[128,1,512]{2,0,1:T(8,128)(2,1)}), bf16[2048,1,512]{2,0,1:T(8,128)(2,1)}) %all-gather.19.cloned.1.call-update) | async-done | bytes 2097168 | tf_op jit(solution)/shard_map/all_gather | solution.py:96
  156.6 2.9 copy.48
  159.5 124.3 %all-gather.15.cloned.1.call-done = bf16[4096,2048]{1,0:T(8,128)(2,1)} async-done(((bf16[256,2048]{1,0:T(8,128)(2,1)}), bf16[4096,2048]{1,0:T(8,128)(2,1)}) %all-gather.15.cloned.1.call-update) | async-done | bytes 16777232 | tf_op jit(solution)/shard_map/all_gather | solution.py:60
  283.8 8.2 %fusion.21 = f32[16,8,16,128]{3,1,2,0:T(8,128)S(1)} fusion(bf16[4096,2048]{1,0:T(8,128)(2,1)} %all-gather.15.cloned.1.call-done, f32[2048]{0:T(1024)S(1)} %convert_element_type.72, bf16[128,4096]{1,0:T(8,128)(2,1)S(1)} %copy-done, f32[4096]{0:T(1024)S(1)} %mul.210, f32[128]{0:T(128)S(1)} %add_rsqrt_fusion.1), kind=kOutput, calls=%fused_computation.38 | convolution fusion | flops 2149842944 | bytes 18899456 | tf_op jit(solution)/shard_map/dot_general | solution.py:58
  293.3 32.3 %all-gather.13.cloned.1.call-done = bf16[2048,512]{0,1:T(8,128)(2,1)} async-done(((bf16[128,512]{0,1:T(8,128)(2,1)}), bf16[2048,512]{0,1:T(8,128)(2,1)}) %all-gather.13.cloned.1.call-update) | async-done | bytes 2097168 | tf_op jit(solution)/shard_map/all_gather | solution.py:95
  325.6 1.1 broadcast_in_dim.105
  326.7 33.3 %while.20 = (s32[]{:T(128)}, f32[4,512]{1,0:T(4,128)S(1)}, f32[4,512]{1,0:T(4,128)S(1)}, f32[4,512,128]{2,1,0:T(8,128)}, s32[16]{0:T(128)S(1)}, /*index=5*/s32[]...) while((s32[]{:T(128)}, f32[4,512]{1,0:T(4,128)S(1)}, ...), condition=%wide.region_10.11_spmd.clone, body=%wide.region_3.10_spmd.clone.sunk | while | flops 551332864 | bytes 27935672 | solution.py:133
  328.7 6.3 %conditional.3 = ((f32[4,512]{1,0:T(4,128)S(1)}, f32[4,512]{1,0:T(4,128)S(1)}, f32[4,512,128]{2,1,0:T(8,128)})) conditional(s32[]{:T(128)} %convert_element_type.117, (f32[4,512]{1,0:T(4,128)S(1)}, f32[4,512]{1,0:T(4,128)S(1)}, f32[4,512,128]{2,1,0:T(8,128)}) %tuple.77, (s32[512]{0:T(512)S(1)}, s32[128]{0:T(128)S(1)}, s32[]{:T(128)}, ...), branch_computations={%region_6.6_spmd, %region_7.9_spmd} | conditional | flops 551292928 | bytes 27925118 | solution.py:131
  328.7 1.1 constant_dynamic-slice_fusion
  330.1 1.0 fusion.2
  331.2 1.0 fusion.4
  332.2 1.8 fusion.8
  334.0 1.0 copy-done.3
  337.0 6.3 %conditional.3 = ((f32[4,512]{1,0:T(4,128)S(1)}, f32[4,512]{1,0:T(4,128)S(1)}, f32[4,512,128]{2,1,0:T(8,128)})) conditional(s32[]{:T(128)} %convert_element_type.117, (f32[4,512]{1,0:T(4,128)S(1)}, f32[4,512]{1,0:T(4,128)S(1)}, f32[4,512,128]{2,1,0:T(8,128)}) %tuple.77, (s32[512]{0:T(512)S(1)}, s32[128]{0:T(128)S(1)}, s32[]{:T(128)}, ...), branch_computations={%region_6.6_spmd, %region_7.9_spmd} | conditional | flops 551292928 | bytes 27925118 | solution.py:131
  337.0 1.2 constant_dynamic-slice_fusion
  338.5 1.0 fusion.2
  339.5 1.0 fusion.4
  340.6 1.8 fusion.8
  342.4 1.0 copy-done.3
  345.4 6.3 %conditional.3 = ((f32[4,512]{1,0:T(4,128)S(1)}, f32[4,512]{1,0:T(4,128)S(1)}, f32[4,512,128]{2,1,0:T(8,128)})) conditional(s32[]{:T(128)} %convert_element_type.117, (f32[4,512]{1,0:T(4,128)S(1)}, f32[4,512]{1,0:T(4,128)S(1)}, f32[4,512,128]{2,1,0:T(8,128)}) %tuple.77, (s32[512]{0:T(512)S(1)}, s32[128]{0:T(128)S(1)}, s32[]{:T(128)}, ...), branch_computations={%region_6.6_spmd, %region_7.9_spmd} | conditional | flops 551292928 | bytes 27925118 | solution.py:131
  345.4 1.1 constant_dynamic-slice_fusion
  346.8 1.0 fusion.2
  347.8 1.0 fusion.4
  348.9 1.8 fusion.8
  350.7 1.0 copy-done.3
  353.7 6.3 %conditional.3 = ((f32[4,512]{1,0:T(4,128)S(1)}, f32[4,512]{1,0:T(4,128)S(1)}, f32[4,512,128]{2,1,0:T(8,128)})) conditional(s32[]{:T(128)} %convert_element_type.117, (f32[4,512]{1,0:T(4,128)S(1)}, f32[4,512]{1,0:T(4,128)S(1)}, f32[4,512,128]{2,1,0:T(8,128)}) %tuple.77, (s32[512]{0:T(512)S(1)}, s32[128]{0:T(128)S(1)}, s32[]{:T(128)}, ...), branch_computations={%region_6.6_spmd, %region_7.9_spmd} | conditional | flops 551292928 | bytes 27925118 | solution.py:131
  353.7 1.1 constant_dynamic-slice_fusion
  355.1 1.0 fusion.2
  356.1 1.0 fusion.4
  357.2 1.8 fusion.8
  359.0 1.0 copy-done.3
  360.0 1.6 divide_convert_fusion
  361.8 94.8 %all-gather.17.cloned.1.call-done = bf16[2048,4096]{1,0:T(8,128)(2,1)} async-done(((bf16[2048,256]{1,0:T(8,128)(2,1)}), bf16[2048,4096]{1,0:T(8,128)(2,1)}) %all-gather.17.cloned.1.call-update) | async-done | bytes 16777232 | tf_op jit(solution)/shard_map/all_gather | solution.py:142
  456.6 9.2 %convolution_convert_fusion = bf16[128,4096]{1,0:T(8,128)(2,1)} fusion(bf16[128,2048]{0,1:T(8,128)(2,1)S(1)} %bitcast.47, bf16[2048,4096]{1,0:T(8,128)(2,1)} %all-gather.17.cloned.1.call-done), kind=kOutput, calls=%fused_computation.31 | convolution fusion | flops 2148007936 | bytes 18350080 | tf_op jit(solution)/shard_map/dot_general | solution.py:140
  465.9 18.7 %reduce-scatter.2.cloned.1.call-done = bf16[128,2048]{1,0:T(8,128)(2,1)} async-done(((bf16[128,4096]{1,0:T(8,128)(2,1)}), bf16[128,2048]{1,0:T(8,128)(2,1)}) %reduce-scatter.2.cloned.1.call-update) | async-done | bytes 524304 | tf_op jit(solution)/shard_map/reduce_scatter | solution.py:145
  484.6 1.3 multiply_reduce_fusion
  485.9 4.9 psum.7
  490.8 2.0 multiply_convert_fusion
  (89 shorter events, 9.4 us)
Async XLA Ops:
  7.2 26.4 %all-gather.9.cloned.1.call-start = ((), (), s32[]{:S(2)}) async-start(), calls=%async_computation.1 | async-start | bytes 1572864 | tf_op jit(solution)/shard_map/all_gather | solution.py:49
  7.9 102.8 %all-gather.11.cloned.1.call-start = ((), (), s32[]{:S(2)}) async-start(), calls=%async_computation.2 | async-start | bytes 8912896 | tf_op jit(solution)/shard_map/all_gather | solution.py:67
  9.9 146.8 %all-gather.19.cloned.1.call-start = ((), (), s32[]{:S(2)}) async-start(), calls=%async_computation.7 | async-start | bytes 2228224 | tf_op jit(solution)/shard_map/all_gather | solution.py:96
  35.1 81.9 %copy-start.4 = (s32[16]{0:T(128)S(1)}, s32[16]{0:T(128)}, u32[]{:S(2)}) copy-start(s32[16]{0:T(128)} %param.14) | copy-start | bytes 196
  115.7 5.2 %copy-start.5 = (bf16[2048]{0:T(1024)(128)(2,1)S(1)}, bf16[2048]{0:T(1024)(128)(2,1)}, u32[]{:S(2)}) copy-start(bf16[2048]{0:T(1024)(128)(2,1)} %param.17) | copy-start | bytes 12292
  116.4 167.4 %all-gather.15.cloned.1.call-start = ((), (), s32[]{:S(2)}) async-start(), calls=%async_computation.4 | async-start | bytes 17825792 | tf_op jit(solution)/shard_map/all_gather | solution.py:60
  117.0 166.8 %copy-start = (bf16[128,4096]{1,0:T(8,128)(2,1)S(1)}, bf16[128,4096]{1,0:T(8,128)(2,1)}, u32[]{:S(2)}) copy-start(bf16[128,4096]{1,0:T(8,128)(2,1)} %all-gather.9.cloned.1.call-done) | copy-start | bytes 3145732
  117.0 208.7 %all-gather.13.cloned.1.call-start = ((), (), s32[]{:S(2)}) async-start(), calls=%async_computation.3 | async-start | bytes 2228224 | tf_op jit(solution)/shard_map/all_gather | solution.py:95
  120.1 336.6 %all-gather.17.cloned.1.call-start = ((), (), s32[]{:S(2)}) async-start(), calls=%async_computation.5 | async-start | bytes 17825792 | tf_op jit(solution)/shard_map/all_gather | solution.py:142
  120.7 363.9 %reduce-scatter.2.cloned.1.call-start = ((), (), s32[]{:S(2)}) async-start(), calls=%async_computation.6 | async-start | bytes 1572864 | tf_op jit(solution)/shard_map/reduce_scatter | solution.py:145
  330.1 2.1 copy-start.2
  334.0 1.0 copy-start.3
  338.4 2.1 copy-start.2
  342.4 1.0 copy-start.3
  346.8 2.1 copy-start.2
  350.7 1.0 copy-start.3
  355.1 2.1 copy-start.2
  359.0 1.0 copy-start.3
  456.6 9.2 %copy-start.6 = (bf16[2048]{0:T(1024)(128)(2,1)S(1)}, bf16[2048]{0:T(1024)(128)(2,1)}, u32[]{:S(2)}) copy-start(bf16[2048]{0:T(1024)(128)(2,1)} %param.21) | copy-start | bytes 12292
  456.6 27.9 %copy-start.1 = (bf16[128,2048]{1,0:T(8,128)(2,1)S(1)}, bf16[128,2048]{1,0:T(8,128)(2,1)}, u32[]{:S(2)}) copy-start(bf16[128,2048]{1,0:T(8,128)(2,1)} %param.13) | copy-start | bytes 1572868
Sparse Core Ops, SparseCore 0:
  9.5 23.9 all-gather.8
  36.3 74.2 all-gather.10
  116.5 40.0 all-gather.18
  158.6 125.1 all-gather.14
  286.4 39.2 all-gather.12
  327.7 128.9 all-gather.16
  466.0 18.5 reduce-scatter.1
where the time goes:
time: 500 us
  waiting for transfers between devices  400 us (80%)
  matrix products  33.6 us (7%)
  other arithmetic  18.1 us (4%)
  local copies, waits for them, and re-layouts  16.7 us (3%)
  between operations  15 us (3%)
  blocking collectives  10.4 us (2%)
  loops' own time  5.46 us (1%)
    all_gather x1, waiting for transfers between devices, per_device(): lax.all_gather(w_query, 'seq', axis=0, tiled=True)  124 us
    all_gather x1, waiting for transfers between devices, per_device(): lax.all_gather(w_out, 'seq', axis=1, tiled=True)  94.8 us
    all_gather x1, waiting for transfers between devices, per_device(): lax.all_gather(key_value_weight, 'seq', axis=0, tiled=True)  75.6 us
    all_gather x1, waiting for transfers between devices, per_device(): value_piece = lax.all_gather(value_rows, 'seq', axis=0, tiled=True)  35.1 us
    all_gather x1, waiting for transfers between devices, per_device(): key_piece = lax.all_gather(rotated_keys, 'seq', axis=0, tiled=True)  32.3 us
    reduce_scatter x1, waiting for transfers between devices, per_device(): lax.psum_scatter(partial_out.astype(jnp.bfloat16), 'tp', scatter_dimensio...  18.7 us
    all_gather x1, waiting for transfers between devices, per_device(): lax.all_gather(hidden_in, 'tp', axis=1, tiled=True)  17.4 us
  transfers between devices with their start and end apart: 7, of which 7 were waited for; matrix products, arithmetic and copies ran while one was open for 9% of the time, Pallas kernels for 0%

commit v1 on v0

--- a/solution.py
+++ b/solution.py
@@ -3,6 +3,7 @@
 import jax.numpy as jnp
 from jax import lax
 from jax.sharding import PartitionSpec as P
+from jax.lax import axis_index, axis_size, ppermute
 
 MODEL_WIDTH = 4096
 HEAD_SIZE = 128
@@ -92,7 +93,15 @@
         jnp.zeros((kv_heads, GROUP * tok_rows), jnp.float32),
         jnp.zeros((kv_heads, GROUP * tok_rows, HEAD_SIZE), jnp.float32),
     )
-    key_piece = lax.all_gather(rotated_keys, "seq", axis=0, tiled=True)
+    axis_total = axis_size("seq")
+    rows = [(dd, (dd + 1) % axis_total) for dd in range(axis_total)]
+    current_arr = [None] * axis_total
+    current_arr[axis_total - 1] = rotated_keys
+    for i0 in range(axis_total - 2, -1, -1):
+        current_arr[i0] = ppermute(current_arr[i0 + 1], "seq", rows)
+    arr_now = jnp.concatenate(current_arr, 0)
+    q_next = (axis_index("seq") + 1) * rotated_keys.shape[0]
+    key_piece = jnp.roll(arr_now, q_next, 0)
     value_piece = lax.all_gather(value_rows, "seq", axis=0, tiled=True)
     count = key_piece.shape[0]
     block = math.gcd(count, 1536)

time: 500 us -> 469 us (0.938)
  waiting for transfers between devices: 400 us -> 366 us
    ppermute x0 -> x15, waiting for transfers between devices: none -> 129 us  [per_device(): current_arr[i0] = ppermute(current_arr[i0 + 1], 'seq', rows)]
    all_gather x1, waiting for transfers between devices: 124 us -> 37.6 us  [per_device(): lax.all_gather(w_query, 'seq', axis=0, tiled=True)]
    all_gather x1, waiting for transfers between devices: 35.1 us -> 0.02 us  [per_device(): value_piece = lax.all_gather(value_rows, 'seq', axis=0, tiled=True)]
    all_gather x1 -> x0, waiting for transfers between devices: 32.3 us -> none  [per_device(): key_piece = lax.all_gather(rotated_keys, 'seq', axis=0, tiled=True)]
    all_gather x1, waiting for transfers between devices: 94.8 us -> 85.9 us  [per_device(): lax.all_gather(w_out, 'seq', axis=1, tiled=True)]
  transfers between devices with their start and end apart: 7 -> 21, of which waited for: 7 -> 20; matrix products, arithmetic and copies ran while one was open for 9% -> 10% of each run, Pallas kernels for 0% -> 0%
where the time goes in v1:
time: 469 us; the launch traced here: 468 us
  waiting for transfers between devices  366 us (78%)
  matrix products  33.6 us (7%)
  local copies, waits for them, and re-layouts  18.7 us (4%)
  other arithmetic  18.2 us (4%)
  between operations  15.2 us (3%)
  blocking collectives  10.4 us (2%)
  loops' own time  5.43 us (1%)
    ppermute x15, waiting for transfers between devices, per_device(): current_arr[i0] = ppermute(current_arr[i0 + 1], 'seq', rows)  129 us
    all_gather x1, waiting for transfers between devices, per_device(): lax.all_gather(w_out, 'seq', axis=1, tiled=True)  85.9 us
    all_gather x1, waiting for transfers between devices, per_device(): lax.all_gather(key_value_weight, 'seq', axis=0, tiled=True)  75.6 us
    all_gather x1, waiting for transfers between devices, per_device(): lax.all_gather(w_query, 'seq', axis=0, tiled=True)  37.6 us
    reduce_scatter x1, waiting for transfers between devices, per_device(): lax.psum_scatter(partial_out.astype(jnp.bfloat16), 'tp', scatter_dimensio...  18.7 us
    all_gather x1, waiting for transfers between devices, per_device(): lax.all_gather(hidden_in, 'tp', axis=1, tiled=True)  17.4 us
  transfers between devices with their start and end apart: 21, of which 20 were waited for; matrix products, arithmetic and copies ran while one was open for 10% of the time, Pallas kernels for 0%

profile of v1, /device:TPU:0, one launch (start us, length us, event | category | flops | bytes accessed | tf_op | source)
XLA Modules:
  0.0 467.9 jit_solution(12692073814429591210)
XLA Ops:
  7.9 1.9 copy.44
  9.9 5.5 %all-gather = bf16[4096]{0:T(1024)(128)(2,1)S(1)} all-gather(bf16[2048]{0:T(1024)(128)(2,1)} %param.15), channel_id=2, replica_groups=mesh['seq'=16,'tp'=2] {'tp'}, dimensions={0}, use_global_device_ids=true | all-gather | bytes 12288 | tf_op jit(solution)/shard_map/all_gather | solution.py:51
  16.1 17.4 %all-gather.8.cloned.1.call-done = bf16[128,4096]{1,0:T(8,128)(2,1)} async-done(((bf16[128,2048]{1,0:T(8,128)(2,1)}), bf16[128,4096]{1,0:T(8,128)(2,1)}) %all-gather.8.cloned.1.call-update) | async-done | bytes 1048592 | tf_op jit(solution)/shard_map/all_gather | solution.py:50
  33.6 1.5 fusion.18
  35.1 75.6 %all-gather.10.cloned.1.call-done = bf16[4096,2,512]{2,0,1:T(8,128)(2,1)} async-done(((bf16[256,2,512]{2,0,1:T(8,128)(2,1)}), bf16[4096,2,512]{2,0,1:T(8,128)(2,1)}) %all-gather.10.cloned.1.call-update) | async-done | bytes 8388624 | tf_op jit(solution)/shard_map/all_gather | solution.py:68
  110.7 5.0 %convolution_add_fusion.1 = f32[128,2,512]{2,0,1:T(8,128)S(1)} fusion(bf16[4096,2,512]{2,0,1:T(8,128)(2,1)} %all-gather.10.cloned.1.call-done, bf16[128,4096]{1,0:T(8,128)(2,1)} %all-gather.8.cloned.1.call-done, f32[4096]{0:T(1024)S(1)} %mul.214, f32[128]{0:T(128)S(1)} %add_rsqrt_fusion.1, f32[2,512]{1,0:T(2,128)S(1)} %convert_element_type.69), kind=kOutput, calls=%fused_computation.39 | convolution fusion | flops 1075970048 | bytes 9982464 | tf_op jit(solution)/shard_map/tr,rkc->tkc/dot_general | solution.py:65
  120.3 7.0 %collective-permute-done = bf16[128,512]{0,1:T(8,128)(2,1)S(1)} collective-permute-done((bf16[128,512]{0,1:T(8,128)(2,1)S(1)}, bf16[128,512]{0,1:T(8,128)(2,1)S(1)}, u32[]{:S(2)}, u32[]{:S(2)}) %collective-permute-start) | collective-permute-done | bytes 131104 | tf_op jit(solution)/shard_map/ppermute | solution.py:101
  127.3 8.0 %collective-permute-done.1 = bf16[128,512]{0,1:T(8,128)(2,1)S(1)} collective-permute-done((bf16[128,512]{0,1:T(8,128)(2,1)S(1)}, bf16[128,512]{0,1:T(8,128)(2,1)S(1)}, u32[]{:S(2)}, u32[]{:S(2)}) %collective-permute-start.1) | collective-permute-done | bytes 131104 | tf_op jit(solution)/shard_map/ppermute | solution.py:101
  135.2 7.1 %collective-permute-done.2 = bf16[128,512]{0,1:T(8,128)(2,1)S(1)} collective-permute-done((bf16[128,512]{0,1:T(8,128)(2,1)S(1)}, bf16[128,512]{0,1:T(8,128)(2,1)S(1)}, u32[]{:S(2)}, u32[]{:S(2)}) %collective-permute-start.2) | collective-permute-done | bytes 131104 | tf_op jit(solution)/shard_map/ppermute | solution.py:101
  142.3 8.5 %collective-permute-done.3 = bf16[128,512]{0,1:T(8,128)(2,1)S(1)} collective-permute-done((bf16[128,512]{0,1:T(8,128)(2,1)S(1)}, bf16[128,512]{0,1:T(8,128)(2,1)S(1)}, u32[]{:S(2)}, u32[]{:S(2)}) %collective-permute-start.3) | collective-permute-done | bytes 131104 | tf_op jit(solution)/shard_map/ppermute | solution.py:101
  150.8 7.3 %collective-permute-done.4 = bf16[128,512]{0,1:T(8,128)(2,1)S(1)} collective-permute-done((bf16[128,512]{0,1:T(8,128)(2,1)S(1)}, bf16[128,512]{0,1:T(8,128)(2,1)S(1)}, u32[]{:S(2)}, u32[]{:S(2)}) %collective-permute-start.4) | collective-permute-done | bytes 131104 | tf_op jit(solution)/shard_map/ppermute | solution.py:101
  158.1 7.1 %collective-permute-done.5 = bf16[128,512]{0,1:T(8,128)(2,1)S(1)} collective-permute-done((bf16[128,512]{0,1:T(8,128)(2,1)S(1)}, bf16[128,512]{0,1:T(8,128)(2,1)S(1)}, u32[]{:S(2)}, u32[]{:S(2)}) %collective-permute-start.5) | collective-permute-done | bytes 131104 | tf_op jit(solution)/shard_map/ppermute | solution.py:101
  165.2 7.2 %collective-permute-done.6 = bf16[128,512]{0,1:T(8,128)(2,1)S(1)} collective-permute-done((bf16[128,512]{0,1:T(8,128)(2,1)S(1)}, bf16[128,512]{0,1:T(8,128)(2,1)S(1)}, u32[]{:S(2)}, u32[]{:S(2)}) %collective-permute-start.6) | collective-permute-done | bytes 131104 | tf_op jit(solution)/shard_map/ppermute | solution.py:101
  172.4 10.0 %collective-permute-done.7 = bf16[128,512]{0,1:T(8,128)(2,1)S(1)} collective-permute-done((bf16[128,512]{0,1:T(8,128)(2,1)S(1)}, bf16[128,512]{0,1:T(8,128)(2,1)S(1)}, u32[]{:S(2)}, u32[]{:S(2)}) %collective-permute-start.7) | collective-permute-done | bytes 131104 | tf_op jit(solution)/shard_map/ppermute | solution.py:101
  182.4 10.0 %collective-permute-done.8 = bf16[128,512]{0,1:T(8,128)(2,1)S(1)} collective-permute-done((bf16[128,512]{0,1:T(8,128)(2,1)S(1)}, bf16[128,512]{0,1:T(8,128)(2,1)S(1)}, u32[]{:S(2)}, u32[]{:S(2)}) %collective-permute-start.8) | collective-permute-done | bytes 131104 | tf_op jit(solution)/shard_map/ppermute | solution.py:101
  192.5 10.0 %collective-permute-done.9 = bf16[128,512]{0,1:T(8,128)(2,1)S(1)} collective-permute-done((bf16[128,512]{0,1:T(8,128)(2,1)S(1)}, bf16[128,512]{0,1:T(8,128)(2,1)S(1)}, u32[]{:S(2)}, u32[]{:S(2)}) %collective-permute-start.9) | collective-permute-done | bytes 131104 | tf_op jit(solution)/shard_map/ppermute | solution.py:101
  202.5 10.0 %collective-permute-done.10 = bf16[128,512]{0,1:T(8,128)(2,1)S(1)} collective-permute-done((bf16[128,512]{0,1:T(8,128)(2,1)S(1)}, bf16[128,512]{0,1:T(8,128)(2,1)S(1)}, u32[]{:S(2)}, u32[]{:S(2)}) %collective-permute-start.10) | collective-permute-done | bytes 131104 | tf_op jit(solution)/shard_map/ppermute | solution.py:101
  212.5 7.2 %collective-permute-done.11 = bf16[128,512]{0,1:T(8,128)(2,1)S(1)} collective-permute-done((bf16[128,512]{0,1:T(8,128)(2,1)S(1)}, bf16[128,512]{0,1:T(8,128)(2,1)S(1)}, u32[]{:S(2)}, u32[]{:S(2)}) %collective-permute-start.11) | collective-permute-done | bytes 131104 | tf_op jit(solution)/shard_map/ppermute | solution.py:101
  219.6 10.0 %collective-permute-done.12 = bf16[128,512]{0,1:T(8,128)(2,1)S(1)} collective-permute-done((bf16[128,512]{0,1:T(8,128)(2,1)S(1)}, bf16[128,512]{0,1:T(8,128)(2,1)S(1)}, u32[]{:S(2)}, u32[]{:S(2)}) %collective-permute-start.12) | collective-permute-done | bytes 131104 | tf_op jit(solution)/shard_map/ppermute | solution.py:101
  229.7 10.0 %collective-permute-done.13 = bf16[128,512]{0,1:T(8,128)(2,1)S(1)} collective-permute-done((bf16[128,512]{0,1:T(8,128)(2,1)S(1)}, bf16[128,512]{0,1:T(8,128)(2,1)S(1)}, u32[]{:S(2)}, u32[]{:S(2)}) %collective-permute-start.13) | collective-permute-done | bytes 131104 | tf_op jit(solution)/shard_map/ppermute | solution.py:101
  240.4 9.4 %collective-permute-done.14 = bf16[128,512]{0,1:T(8,128)(2,1)S(1)} collective-permute-done((bf16[128,512]{0,1:T(8,128)(2,1)S(1)}, bf16[128,512]{0,1:T(8,128)(2,1)S(1)}, u32[]{:S(2)}, u32[]{:S(2)}) %collective-permute-start.14) | collective-permute-done | bytes 131104 | tf_op jit(solution)/shard_map/ppermute | solution.py:101
  251.4 4.1 copy.48
  255.5 37.6 %all-gather.12.cloned.1.call-done = bf16[4096,2048]{1,0:T(8,128)(2,1)} async-done(((bf16[256,2048]{1,0:T(8,128)(2,1)}), bf16[4096,2048]{1,0:T(8,128)(2,1)}) %all-gather.12.cloned.1.call-update) | async-done | bytes 16777232 | tf_op jit(solution)/shard_map/all_gather | solution.py:61
  293.2 8.2 %fusion.21 = f32[16,8,16,128]{3,1,2,0:T(8,128)S(1)} fusion(bf16[4096,2048]{1,0:T(8,128)(2,1)} %all-gather.12.cloned.1.call-done, f32[2048]{0:T(1024)S(1)} %convert_element_type.72, bf16[128,4096]{1,0:T(8,128)(2,1)S(1)} %copy-done, f32[4096]{0:T(1024)S(1)} %mul.214, f32[128]{0:T(128)S(1)} %add_rsqrt_fusion.1), kind=kOutput, calls=%fused_computation.38 | convolution fusion | flops 2149842944 | bytes 18899456 | tf_op jit(solution)/shard_map/dot_general | solution.py:59
  302.7 1.1 broadcast_in_dim.105
  303.7 33.4 %while.20 = (s32[]{:T(128)}, f32[4,512]{1,0:T(4,128)S(1)}, f32[4,512]{1,0:T(4,128)S(1)}, f32[4,512,128]{2,1,0:T(8,128)}, s32[16]{0:T(128)S(1)}, /*index=5*/s32[]...) while((s32[]{:T(128)}, f32[4,512]{1,0:T(4,128)S(1)}, ...), condition=%wide.region_10.11_spmd.clone, body=%wide.region_3.10_spmd.clone.sunk | while | flops 551332864 | bytes 27935672 | solution.py:142
  305.8 6.3 %conditional.3 = ((f32[4,512]{1,0:T(4,128)S(1)}, f32[4,512]{1,0:T(4,128)S(1)}, f32[4,512,128]{2,1,0:T(8,128)})) conditional(s32[]{:T(128)} %convert_element_type.117, (f32[4,512]{1,0:T(4,128)S(1)}, f32[4,512]{1,0:T(4,128)S(1)}, f32[4,512,128]{2,1,0:T(8,128)}) %tuple.77, (s32[512]{0:T(512)S(1)}, s32[128]{0:T(128)S(1)}, s32[]{:T(128)}, ...), branch_computations={%region_6.6_spmd, %region_7.9_spmd} | conditional | flops 551292928 | bytes 27925118 | solution.py:140
  305.8 1.2 constant_dynamic-slice_fusion
  308.2 1.0 fusion.4
  309.3 1.8 fusion.8
  314.1 6.3 %conditional.3 = ((f32[4,512]{1,0:T(4,128)S(1)}, f32[4,512]{1,0:T(4,128)S(1)}, f32[4,512,128]{2,1,0:T(8,128)})) conditional(s32[]{:T(128)} %convert_element_type.117, (f32[4,512]{1,0:T(4,128)S(1)}, f32[4,512]{1,0:T(4,128)S(1)}, f32[4,512,128]{2,1,0:T(8,128)}) %tuple.77, (s32[512]{0:T(512)S(1)}, s32[128]{0:T(128)S(1)}, s32[]{:T(128)}, ...), branch_computations={%region_6.6_spmd, %region_7.9_spmd} | conditional | flops 551292928 | bytes 27925118 | solution.py:140
  314.1 1.1 constant_dynamic-slice_fusion
  316.6 1.0 fusion.4
  317.6 1.8 fusion.8
  322.5 6.3 %conditional.3 = ((f32[4,512]{1,0:T(4,128)S(1)}, f32[4,512]{1,0:T(4,128)S(1)}, f32[4,512,128]{2,1,0:T(8,128)})) conditional(s32[]{:T(128)} %convert_element_type.117, (f32[4,512]{1,0:T(4,128)S(1)}, f32[4,512]{1,0:T(4,128)S(1)}, f32[4,512,128]{2,1,0:T(8,128)}) %tuple.77, (s32[512]{0:T(512)S(1)}, s32[128]{0:T(128)S(1)}, s32[]{:T(128)}, ...), branch_computations={%region_6.6_spmd, %region_7.9_spmd} | conditional | flops 551292928 | bytes 27925118 | solution.py:140
  322.5 1.1 constant_dynamic-slice_fusion
  324.9 1.0 fusion.4
  326.0 1.8 fusion.8
  330.8 6.3 %conditional.3 = ((f32[4,512]{1,0:T(4,128)S(1)}, f32[4,512]{1,0:T(4,128)S(1)}, f32[4,512,128]{2,1,0:T(8,128)})) conditional(s32[]{:T(128)} %convert_element_type.117, (f32[4,512]{1,0:T(4,128)S(1)}, f32[4,512]{1,0:T(4,128)S(1)}, f32[4,512,128]{2,1,0:T(8,128)}) %tuple.77, (s32[512]{0:T(512)S(1)}, s32[128]{0:T(128)S(1)}, s32[]{:T(128)}, ...), branch_computations={%region_6.6_spmd, %region_7.9_spmd} | conditional | flops 551292928 | bytes 27925118 | solution.py:140
  330.8 1.1 constant_dynamic-slice_fusion
  334.3 1.8 fusion.8
  337.1 1.6 divide_convert_fusion
  339.0 85.9 %all-gather.14.cloned.1.call-done = bf16[2048,4096]{1,0:T(8,128)(2,1)} async-done(((bf16[2048,256]{1,0:T(8,128)(2,1)}), bf16[2048,4096]{1,0:T(8,128)(2,1)}) %all-gather.14.cloned.1.call-update) | async-done | bytes 16777232 | tf_op jit(solution)/shard_map/all_gather | solution.py:151
  424.9 9.2 %convolution_convert_fusion = bf16[128,4096]{1,0:T(8,128)(2,1)} fusion(bf16[128,2048]{0,1:T(8,128)(2,1)S(1)} %bitcast.47, bf16[2048,4096]{1,0:T(8,128)(2,1)} %all-gather.14.cloned.1.call-done), kind=kOutput, calls=%fused_computation.31 | convolution fusion | flops 2148007936 | bytes 18350080 | tf_op jit(solution)/shard_map/dot_general | solution.py:149
  434.1 18.7 %reduce-scatter.2.cloned.1.call-done = bf16[128,2048]{1,0:T(8,128)(2,1)} async-done(((bf16[128,4096]{1,0:T(8,128)(2,1)}), bf16[128,2048]{1,0:T(8,128)(2,1)}) %reduce-scatter.2.cloned.1.call-update) | async-done | bytes 524304 | tf_op jit(solution)/shard_map/reduce_scatter | solution.py:154
  452.8 1.3 multiply_reduce_fusion
  454.1 4.9 %psum.7 = f32[128]{0:T(128)S(1)} all-reduce(f32[128]{0:T(128)S(1)} %multiply_reduce_fusion), channel_id=1, replica_groups=mesh['seq'=16,'tp'=2] {'tp'}, use_global_device_ids=true, to_apply=%region_13.14 | all-reduce | flops 128 | bytes 1024 | tf_op jit(solution)/shard_map/psum | solution.py:159
  459.1 2.0 multiply_convert_fusion
  (149 shorter events, 22.2 us)
Async XLA Ops:
  7.2 26.4 %all-gather.8.cloned.1.call-start = ((), (), s32[]{:S(2)}) async-start(), calls=%async_computation.1 | async-start | bytes 1572864 | tf_op jit(solution)/shard_map/all_gather | solution.py:50
  7.9 102.8 %all-gather.10.cloned.1.call-start = ((), (), s32[]{:S(2)}) async-start(), calls=%async_computation.2 | async-start | bytes 8912896 | tf_op jit(solution)/shard_map/all_gather | solution.py:68
  9.9 241.6 %all-gather.16.cloned.1.call-start = ((), (), s32[]{:S(2)}) async-start(), calls=%async_computation.6 | async-start | bytes 2228224 | tf_op jit(solution)/shard_map/all_gather | solution.py:105
  35.1 82.5 %copy-start.4 = (s32[16]{0:T(128)S(1)}, s32[16]{0:T(128)}, u32[]{:S(2)}) copy-start(s32[16]{0:T(128)} %param.14) | copy-start | bytes 196
  115.7 124.0 %copy-start.5 = (bf16[2048]{0:T(1024)(128)(2,1)S(1)}, bf16[2048]{0:T(1024)(128)(2,1)}, u32[]{:S(2)}) copy-start(bf16[2048]{0:T(1024)(128)(2,1)} %param.17) | copy-start | bytes 12292
  116.4 176.8 %all-gather.12.cloned.1.call-start = ((), (), s32[]{:S(2)}) async-start(), calls=%async_computation.3 | async-start | bytes 17825792 | tf_op jit(solution)/shard_map/all_gather | solution.py:61
  117.0 307.9 %all-gather.14.cloned.1.call-start = ((), (), s32[]{:S(2)}) async-start(), calls=%async_computation.4 | async-start | bytes 17825792 | tf_op jit(solution)/shard_map/all_gather | solution.py:151
  117.6 335.3 %reduce-scatter.2.cloned.1.call-start = ((), (), s32[]{:S(2)}) async-start(), calls=%async_computation.5 | async-start | bytes 1572864 | tf_op jit(solution)/shard_map/reduce_scatter | solution.py:154
  120.0 7.3 %collective-permute-start = (bf16[128,512]{0,1:T(8,128)(2,1)S(1)}, bf16[128,512]{0,1:T(8,128)(2,1)S(1)}, u32[]{:S(2)}, u32[]{:S(2)}) collective-permute-start(bf16[128,512]{0,1:T(8,128)(2,1)S(1)} %bitcast.52), channel_id=1, source_target_pairs={{0,2},{2,4},{4,6},{6,8},{8,10},{10,12},{12,14},{14,16},{16,18},{18... | collective-permute-start | bytes 393224 | tf_op jit(solution)/shard_map/ppermute | solution.py:101
  127.3 8.0 %collective-permute-start.1 = (bf16[128,512]{0,1:T(8,128)(2,1)S(1)}, bf16[128,512]{0,1:T(8,128)(2,1)S(1)}, u32[]{:S(2)}, u32[]{:S(2)}) collective-permute-start(bf16[128,512]{0,1:T(8,128)(2,1)S(1)} %collective-permute-done), channel_id=1, source_target_pairs={{0,2},{2,4},{4,6},{6,8},{8,10},{10,12},{12,14},{14,16},{16,18},{18... | collective-permute-start | bytes 393224 | tf_op jit(solution)/shard_map/ppermute | solution.py:101
  135.2 7.1 %collective-permute-start.2 = (bf16[128,512]{0,1:T(8,128)(2,1)S(1)}, bf16[128,512]{0,1:T(8,128)(2,1)S(1)}, u32[]{:S(2)}, u32[]{:S(2)}) collective-permute-start(bf16[128,512]{0,1:T(8,128)(2,1)S(1)} %collective-permute-done.1), channel_id=1, source_target_pairs={{0,2},{2,4},{4,6},{6,8},{8,10},{10,12},{12,14},{14,16},{16,18},{18... | collective-permute-start | bytes 393224 | tf_op jit(solution)/shard_map/ppermute | solution.py:101
  142.3 8.5 %collective-permute-start.3 = (bf16[128,512]{0,1:T(8,128)(2,1)S(1)}, bf16[128,512]{0,1:T(8,128)(2,1)S(1)}, u32[]{:S(2)}, u32[]{:S(2)}) collective-permute-start(bf16[128,512]{0,1:T(8,128)(2,1)S(1)} %collective-permute-done.2), channel_id=1, source_target_pairs={{0,2},{2,4},{4,6},{6,8},{8,10},{10,12},{12,14},{14,16},{16,18},{18... | collective-permute-start | bytes 393224 | tf_op jit(solution)/shard_map/ppermute | solution.py:101
  150.8 7.3 %collective-permute-start.4 = (bf16[128,512]{0,1:T(8,128)(2,1)S(1)}, bf16[128,512]{0,1:T(8,128)(2,1)S(1)}, u32[]{:S(2)}, u32[]{:S(2)}) collective-permute-start(bf16[128,512]{0,1:T(8,128)(2,1)S(1)} %collective-permute-done.3), channel_id=1, source_target_pairs={{0,2},{2,4},{4,6},{6,8},{8,10},{10,12},{12,14},{14,16},{16,18},{18... | collective-permute-start | bytes 393224 | tf_op jit(solution)/shard_map/ppermute | solution.py:101
  158.1 7.1 %collective-permute-start.5 = (bf16[128,512]{0,1:T(8,128)(2,1)S(1)}, bf16[128,512]{0,1:T(8,128)(2,1)S(1)}, u32[]{:S(2)}, u32[]{:S(2)}) collective-permute-start(bf16[128,512]{0,1:T(8,128)(2,1)S(1)} %collective-permute-done.4), channel_id=1, source_target_pairs={{0,2},{2,4},{4,6},{6,8},{8,10},{10,12},{12,14},{14,16},{16,18},{18... | collective-permute-start | bytes 393224 | tf_op jit(solution)/shard_map/ppermute | solution.py:101
  165.2 7.2 %collective-permute-start.6 = (bf16[128,512]{0,1:T(8,128)(2,1)S(1)}, bf16[128,512]{0,1:T(8,128)(2,1)S(1)}, u32[]{:S(2)}, u32[]{:S(2)}) collective-permute-start(bf16[128,512]{0,1:T(8,128)(2,1)S(1)} %collective-permute-done.5), channel_id=1, source_target_pairs={{0,2},{2,4},{4,6},{6,8},{8,10},{10,12},{12,14},{14,16},{16,18},{18... | collective-permute-start | bytes 393224 | tf_op jit(solution)/shard_map/ppermute | solution.py:101
  172.4 10.0 %collective-permute-start.7 = (bf16[128,512]{0,1:T(8,128)(2,1)S(1)}, bf16[128,512]{0,1:T(8,128)(2,1)S(1)}, u32[]{:S(2)}, u32[]{:S(2)}) collective-permute-start(bf16[128,512]{0,1:T(8,128)(2,1)S(1)} %collective-permute-done.6), channel_id=1, source_target_pairs={{0,2},{2,4},{4,6},{6,8},{8,10},{10,12},{12,14},{14,16},{16,18},{18... | collective-permute-start | bytes 393224 | tf_op jit(solution)/shard_map/ppermute | solution.py:101
  182.4 10.0 %collective-permute-start.8 = (bf16[128,512]{0,1:T(8,128)(2,1)S(1)}, bf16[128,512]{0,1:T(8,128)(2,1)S(1)}, u32[]{:S(2)}, u32[]{:S(2)}) collective-permute-start(bf16[128,512]{0,1:T(8,128)(2,1)S(1)} %collective-permute-done.7), channel_id=1, source_target_pairs={{0,2},{2,4},{4,6},{6,8},{8,10},{10,12},{12,14},{14,16},{16,18},{18... | collective-permute-start | bytes 393224 | tf_op jit(solution)/shard_map/ppermute | solution.py:101
  192.5 10.0 %collective-permute-start.9 = (bf16[128,512]{0,1:T(8,128)(2,1)S(1)}, bf16[128,512]{0,1:T(8,128)(2,1)S(1)}, u32[]{:S(2)}, u32[]{:S(2)}) collective-permute-start(bf16[128,512]{0,1:T(8,128)(2,1)S(1)} %collective-permute-done.8), channel_id=1, source_target_pairs={{0,2},{2,4},{4,6},{6,8},{8,10},{10,12},{12,14},{14,16},{16,18},{18... | collective-permute-start | bytes 393224 | tf_op jit(solution)/shard_map/ppermute | solution.py:101
  202.5 10.0 %collective-permute-start.10 = (bf16[128,512]{0,1:T(8,128)(2,1)S(1)}, bf16[128,512]{0,1:T(8,128)(2,1)S(1)}, u32[]{:S(2)}, u32[]{:S(2)}) collective-permute-start(bf16[128,512]{0,1:T(8,128)(2,1)S(1)} %collective-permute-done.9), channel_id=1, source_target_pairs={{0,2},{2,4},{4,6},{6,8},{8,10},{10,12},{12,14},{14,16},{16,18},{18... | collective-permute-start | bytes 393224 | tf_op jit(solution)/shard_map/ppermute | solution.py:101
  212.5 7.2 %collective-permute-start.11 = (bf16[128,512]{0,1:T(8,128)(2,1)S(1)}, bf16[128,512]{0,1:T(8,128)(2,1)S(1)}, u32[]{:S(2)}, u32[]{:S(2)}) collective-permute-start(bf16[128,512]{0,1:T(8,128)(2,1)S(1)} %collective-permute-done.10), channel_id=1, source_target_pairs={{0,2},{2,4},{4,6},{6,8},{8,10},{10,12},{12,14},{14,16},{16,18},{18... | collective-permute-start | bytes 393224 | tf_op jit(solution)/shard_map/ppermute | solution.py:101
  219.6 10.0 %collective-permute-start.12 = (bf16[128,512]{0,1:T(8,128)(2,1)S(1)}, bf16[128,512]{0,1:T(8,128)(2,1)S(1)}, u32[]{:S(2)}, u32[]{:S(2)}) collective-permute-start(bf16[128,512]{0,1:T(8,128)(2,1)S(1)} %collective-permute-done.11), channel_id=1, source_target_pairs={{0,2},{2,4},{4,6},{6,8},{8,10},{10,12},{12,14},{14,16},{16,18},{18... | collective-permute-start | bytes 393224 | tf_op jit(solution)/shard_map/ppermute | solution.py:101
  229.7 10.0 %collective-permute-start.13 = (bf16[128,512]{0,1:T(8,128)(2,1)S(1)}, bf16[128,512]{0,1:T(8,128)(2,1)S(1)}, u32[]{:S(2)}, u32[]{:S(2)}) collective-permute-start(bf16[128,512]{0,1:T(8,128)(2,1)S(1)} %collective-permute-done.12), channel_id=1, source_target_pairs={{0,2},{2,4},{4,6},{6,8},{8,10},{10,12},{12,14},{14,16},{16,18},{18... | collective-permute-start | bytes 393224 | tf_op jit(solution)/shard_map/ppermute | solution.py:101
  239.7 10.0 %collective-permute-start.14 = (bf16[128,512]{0,1:T(8,128)(2,1)S(1)}, bf16[128,512]{0,1:T(8,128)(2,1)S(1)}, u32[]{:S(2)}, u32[]{:S(2)}) collective-permute-start(bf16[128,512]{0,1:T(8,128)(2,1)S(1)} %collective-permute-done.13), channel_id=1, source_target_pairs={{0,2},{2,4},{4,6},{6,8},{8,10},{10,12},{12,14},{14,16},{16,18},{18... | collective-permute-start | bytes 393224 | tf_op jit(solution)/shard_map/ppermute | solution.py:101
  251.2 42.0 %copy-start = (bf16[128,4096]{1,0:T(8,128)(2,1)S(1)}, bf16[128,4096]{1,0:T(8,128)(2,1)}, u32[]{:S(2)}) copy-start(bf16[128,4096]{1,0:T(8,128)(2,1)} %all-gather.8.cloned.1.call-done) | copy-start | bytes 3145732
  307.2 2.1 copy-start.2
  311.1 1.0 copy-start.3
  315.5 2.1 copy-start.2
  319.4 1.0 copy-start.3
  323.8 2.1 copy-start.2
  327.8 1.0 copy-start.3
  332.2 2.1 copy-start.2
  336.1 1.0 copy-start.3
  424.9 9.2 %copy-start.6 = (bf16[2048]{0:T(1024)(128)(2,1)S(1)}, bf16[2048]{0:T(1024)(128)(2,1)}, u32[]{:S(2)}) copy-start(bf16[2048]{0:T(1024)(128)(2,1)} %param.21) | copy-start | bytes 12292
  424.9 27.9 %copy-start.1 = (bf16[128,2048]{1,0:T(8,128)(2,1)S(1)}, bf16[128,2048]{1,0:T(8,128)(2,1)}, u32[]{:S(2)}) copy-start(bf16[128,2048]{1,0:T(8,128)(2,1)} %param.13) | copy-start | bytes 1572868
Sparse Core Ops, SparseCore 0:
  9.5 23.9 all-gather.7
  36.3 74.2 all-gather.9
  116.5 41.7 all-gather.15
  160.3 132.7 all-gather.11
  295.2 129.6 all-gather.13
  434.2 18.5 reduce-scatter.1
